TPU v7x, 32 devices: a whole 2x2x4 slice. The times are simulated.
32 devices in a mesh: row: 4 (over z), col: 8 (over y, x, core).
Axes of the slice: x: 2, y: 2, z: 4, core: 2. Of those that a mesh axis runs over, the one named last changes fastest.
Arguments:
- response_coeffs: float32 [3, 8192, 1024], P(None, ('row', 'col')), may hold values from -6 to 6
- occupied_coeffs: float32 [8192, 1024], P(('row', 'col')), may hold values from -0.1875 to 0.1875
Outputs:
- density: float32 [3, 8192, 8192], P(None, 'row', 'col')
All inputs are finite; a program needn't handle non-finite values.
Results may differ from a plain program's by a relative error of at most 0.0003.
Values sent between devices are 32-bit elements; how exact they have to be, the bound alone decides.
A program may use at most 256 MiB of HBM per device.

v0:
```python
import jax
import jax.numpy as jnp
from jax import lax
from jax.sharding import PartitionSpec as P

SLICE_PAIRS = ((0, 0), (0, 1), (1, 0))


def partner(value, axis, stride):
    mask = 2**stride
    pairs = [(source, source ^ mask) for source in range(lax.axis_size(axis))]
    return lax.ppermute(value, axis, pairs)


def split_slices(values):
    leading = lax.optimization_barrier(values.astype(jnp.bfloat16))
    remainder = values - leading.astype(jnp.float32)
    trailing = lax.optimization_barrier(remainder.astype(jnp.bfloat16))
    return [leading, trailing]


def contribute(row_slices, column_slices, perturbations):
    accumulated = jnp.zeros(
        (perturbations, row_slices[0].shape[1], column_slices[0].shape[1]), jnp.float32
    )
    for left_index, right_index in SLICE_PAIRS:
        forward_term = jnp.einsum(
            "kro,co->krc",
            row_slices[left_index][:perturbations],
            column_slices[right_index][perturbations],
            preferred_element_type=jnp.float32,
        )
        mirror_term = jnp.einsum(
            "ro,kco->krc",
            row_slices[right_index][perturbations],
            column_slices[left_index][:perturbations],
            preferred_element_type=jnp.float32,
        )
        accumulated = accumulated + forward_term + mirror_term
    return accumulated


def relay_columns(stacked, perturbations):
    rows_total = lax.axis_size("row")
    columns_total = lax.axis_size("col")
    col_index = lax.axis_index("col")
    shard_rows = stacked.shape[1]
    orbitals = stacked.shape[2]
    half_rows = shard_rows // 2
    swap_bit = rows_total.bit_length() - 1
    own_first = stacked[:, :half_rows]
    partner_second = partner(stacked[:, half_rows:], "col", swap_bit)
    even_first = col_index // rows_total == 0
    leading = jnp.where(even_first, own_first, partner_second)
    trailing = jnp.where(even_first, partner_second, own_first)
    paired = jnp.concatenate([leading, trailing], axis=1)
    gathered = lax.all_gather(paired, "row", axis=1, tiled=True)
    regrouped = lax.all_to_all(gathered, "col", split_axis=1, concat_axis=1, tiled=True)
    shaped = regrouped.reshape(perturbations + 1, 2, rows_total, half_rows, orbitals)
    flipped = shaped[:, ::-1]
    ordered = jnp.where(col_index % 2 == 0, shaped, flipped)
    return jnp.swapaxes(ordered, 1, 2).reshape(
        perturbations + 1, columns_total * half_rows, orbitals
    )


def shards(response_coeffs, occupied_coeffs):
    perturbations = response_coeffs.shape[0]
    stacked = jnp.concatenate([response_coeffs, occupied_coeffs[None]], axis=0)
    column_panel = relay_columns(stacked, perturbations)
    column_slices = split_slices(column_panel)
    return contribute(
        split_slices(lax.all_gather(stacked, "col", axis=1, tiled=True)),
        column_slices,
        perturbations,
    )


def solution(mesh):
    return jax.shard_map(
        shards,
        mesh=mesh,
        in_specs=(P(None, ("row", "col"), None), P(("row", "col"), None)),
        out_specs=P(None, "row", "col"),
        check_vma=False,
    )
```

profile of v0, /device:TPU:0, one launch (start us, length us, event | category | flops | bytes accessed | tf_op | source)
XLA Modules:
  0.0 913.4 jit_solution(8449333909172042322)
XLA Ops:
  6.5 0.0 copy-start.2
  6.5 0.0 all-gather.5.cloned.1.call-start
  6.5 3.2 fusion.7
  9.8 3.0 collective-permute-start
  12.8 45.9 %collective-permute-done = f32[4,128,1024]{2,1,0:T(8,128)} collective-permute-done((f32[4,128,1024]{2,1,0:T(8,128)}, f32[4,128,1024]{2,1,0:T(8,128)}, u32[]{:S(2)}, u32[]{:S(2)}) %collective-permute-start) | collective-permute-done | bytes 2097184 | tf_op jit(solution)/shard_map/ppermute | solution.py:12
  58.7 0.0 copy-done.2
  58.7 2.4 broadcast_select_fusion.1
  61.1 2.5 pad_maximum_fusion.1
  63.6 0.0 all-gather.5.cloned.1.call-update
  63.7 0.0 all-gather.3.cloned.1.call-start
  63.7 3.7 pad_maximum_fusion
  67.4 0.0 all-gather.3.cloned.1.call-update
  67.4 284.7 %all-gather.5.cloned.1.call-done = f32[4,1024,1024]{2,1,0:T(8,128)} async-done(((f32[4,256,1024]{2,1,0:T(8,128)}), f32[4,1024,1024]{2,1,0:T(8,128)}) %all-gather.5.cloned.1.call-update) | async-done | bytes 16777232 | tf_op jit(solution)/shard_map/all_gather | solution.py:57
  352.1 21.6 %copy.8 = f32[4,1024,1024]{2,0,1:T(4,128)} copy(f32[4,1024,1024]{2,1,0:T(8,128)} %all-gather.5.cloned.1.call-done) | data formatting | bytes 33554432 | tf_op jit(solution)/shard_map/all_gather | solution.py:57
  373.7 6.0 all-to-all-start
  379.7 302.3 %all-to-all-done = f32[4,1024,1024]{2,0,1:T(4,128)} async-done(((f32[4,1024,1024]{2,0,1:T(4,128)}), f32[4,1024,1024]{2,0,1:T(4,128)}, u32[]{:S(2)}, u32[]{:S(2)}) %all-to-all-start) | async-done | bytes 16777248 | tf_op jit(solution)/shard_map/all_to_all | solution.py:58
  682.0 15.2 %copy.10 = f32[4,2,4,128,1024]{4,3,1,2,0:T(8,128)S(1)} copy(f32[4,2,4,128,1024]{4,0,3,2,1:T(4,128)} %bitcast.1) | data formatting | bytes 33554432 | tf_op jit(solution)/shard_map/reshape | solution.py:59
  697.2 3.4 reverse_select_fusion
  700.6 2.4 bitcast_convert_fusion
  703.1 0.0 copy-start.1
  703.1 3.2 copy-done.1
  706.3 6.3 fusion.2
  712.6 0.0 all-gather.3.cloned.1.call-done
  712.6 12.1 %convert_element_type.18 = bf16[4,2048,1024]{2,1,0:T(8,128)(2,1)S(1)} convert(f32[4,2048,1024]{2,1,0:T(8,128)} %all-gather.3.cloned.1.call-done) | non-fusion elementwise | flops 8388608 | bytes 50331648 | tf_op jit(solution)/shard_map/convert_element_type | solution.py:16
  724.7 0.0 copy-start
  724.7 5.8 copy-done
  730.5 19.0 %fusion.4 = f32[3,1024,2048]{1,2,0:T(8,128)} fusion(bf16[4,1024,1024]{2,1,0:T(8,128)(2,1)} %fusion.2, bf16[4,2048,1024]{2,1,0:T(8,128)(2,1)S(1)} %convert_element_type.18), kind=kOutput, calls=%fused_computation.19 | convolution fusion | flops 12884901888 | bytes 37748736 | tf_op jit(solution)/shard_map/ro,kco->krc/dot_general | solution.py:33
  749.5 22.0 %fusion.8 = f32[3,2048,1024]{2,1,0:T(8,128)} fusion(bf16[4,2048,1024]{2,1,0:T(8,128)(2,1)} %copy-done, bf16[4,1024,1024]{2,1,0:T(8,128)(2,1)} %fusion.2), kind=kOutput, calls=%fused_computation.24 | convolution fusion | flops 12884901888 | bytes 44040192 | tf_op jit(solution)/shard_map/kro,co->krc/dot_general | solution.py:27
  771.5 0.0 slice-start
  771.5 0.0 slice-start.1
  771.5 21.8 %fusion.9 = f32[3,2048,1024]{2,1,0:T(8,128)} fusion(bf16[4,2048,1024]{2,1,0:T(8,128)(2,1)} %copy-done, bf16[4,1024,1024]{2,1,0:T(8,128)(2,1)} %copy-done.1), kind=kOutput, calls=%fused_computation.26 | convolution fusion | flops 12884901888 | bytes 44040192 | tf_op jit(solution)/shard_map/kro,co->krc/dot_general | solution.py:27
  793.3 0.0 slice-start.2
  793.3 0.0 slice-start.3
  793.3 20.0 %fusion.5 = f32[3,1024,2048]{1,2,0:T(8,128)} fusion(bf16[4,1024,1024]{2,1,0:T(8,128)(2,1)} %copy-done.1, bf16[4,2048,1024]{2,1,0:T(8,128)(2,1)} %copy-done), kind=kOutput, calls=%fused_computation.20 | convolution fusion | flops 12884901888 | bytes 37748736 | tf_op jit(solution)/shard_map/ro,kco->krc/dot_general | solution.py:33
  813.3 0.0 slice-done
  813.3 0.0 slice-done.1
  813.3 0.0 slice-done.2
  813.3 0.0 slice-done.3
  813.3 19.5 %subtract_convert_fusion = bf16[4,2048,1024]{2,1,0:T(8,128)(2,1)} fusion(f32[4,2048,1024]{2,1,0:T(8,128)} %all-gather.3.cloned.1.call-done, bf16[4,2048,1024]{2,1,0:T(8,128)(2,1)S(1)} %bitcast.54), kind=kLoop, calls=%fused_computation | loop fusion | flops 25165824 | bytes 67108864 | tf_op jit(solution)/shard_map/convert_element_type | solution.py:18
  832.8 20.0 %fusion.3 = f32[3,1024,2048]{1,2,0:T(8,128)} fusion(bf16[4,1024,1024]{2,1,0:T(8,128)(2,1)} %copy-done.1, bf16[4,2048,1024]{2,1,0:T(8,128)(2,1)} %subtract_convert_fusion), kind=kOutput, calls=%fused_computation.16 | convolution fusion | flops 12884901888 | bytes 37748736 | tf_op jit(solution)/shard_map/ro,kco->krc/dot_general | solution.py:33
  852.8 53.5 %bitcast_add_fusion = f32[3,2048,1024]{2,1,0:T(8,128)} fusion(f32[3,1024,2048]{1,2,0:T(8,128)} %fusion.4, f32[3,1024,2048]{1,2,0:T(8,128)} %fusion.3, f32[3,2048,1024]{2,1,0:T(8,128)} %fusion.8, f32[3,2048,1024]{2,1,0:T(8,128)} %fusion.9, f32[3,1024,2048]{1,2,0:T(8,128)} %fusion.5, bf16[4,2048,1024]{2,1,0:T(8,128)(2,1)} %subtract_convert_fusion, ...), kind=kOutput, calls=%fused_computation.1 | convolution fusion | flops 12916359168 | bytes 169869312 | tf_op jit(solution)/shard_map/kro,co->krc/dot_general | solution.py:27
  (1 shorter events, 0.0 us)
Async XLA Ops:
  6.5 52.2 %copy-start.2 = (f32[3,256,1024]{2,1,0:T(8,128)S(1)}, f32[3,256,1024]{2,1,0:T(8,128)}, u32[]{:S(2)}) copy-start(f32[3,256,1024]{2,1,0:T(8,128)} %param.2) | copy-start | bytes 9437188
  6.5 345.5 %all-gather.5.cloned.1.call-start = ((), (), s32[]{:S(2)}) async-start(), calls=%async_computation.2 | async-start | bytes 20971520 | tf_op jit(solution)/shard_map/all_gather | solution.py:57
  9.8 48.9 %collective-permute-start = (f32[4,128,1024]{2,1,0:T(8,128)}, f32[4,128,1024]{2,1,0:T(8,128)}, u32[]{:S(2)}, u32[]{:S(2)}) collective-permute-start(f32[4,128,1024]{2,1,0:T(8,128)} %fusion.7), channel_id=1, source_target_pairs={{0,4},{1,5},{2,6},{3,7},{4,0},{5,1},{6,2},{7,3},{8,12},{9,13},{10,... | collective-permute-start | bytes 6291464 | tf_op jit(solution)/shard_map/ppermute | solution.py:12
  63.7 648.9 %all-gather.3.cloned.1.call-start = ((), (), s32[]{:S(2)}) async-start(), calls=%async_computation.1 | async-start | bytes 37748736 | tf_op jit(solution)/shard_map/all_gather | solution.py:73
  373.7 308.3 %all-to-all-start = ((f32[4,1024,1024]{2,0,1:T(4,128)}), f32[4,1024,1024]{2,0,1:T(4,128)}, u32[]{:S(2)}, u32[]{:S(2)}) async-start(f32[4,1024,1024]{2,0,1:T(4,128)} %copy.8), calls=%async_computation | async-start | bytes 33554432 | tf_op jit(solution)/shard_map/all_to_all | solution.py:58
  703.1 3.2 copy-start.1
  724.7 5.8 copy-start
  771.5 41.8 %slice-start = ((s8[16777216]{0:T(1024)(128)(4,1)}), s8[4194304]{0:T(1024)(128)(4,1)S(1)}, s32[]{:S(2)}) async-start(s8[16777216]{0:T(1024)(128)(4,1)} %bitcast.53), calls=%async_computation.3 | async-start | bytes 8388608
  771.5 41.8 %slice-start.1 = ((s8[16777216]{0:T(1024)(128)(4,1)}), s8[4194304]{0:T(1024)(128)(4,1)S(1)}, s32[]{:S(2)}) async-start(s8[16777216]{0:T(1024)(128)(4,1)} %bitcast.53), calls=%async_computation.4 | async-start | bytes 8388608
  793.3 20.0 %slice-start.2 = ((s8[16777216]{0:T(1024)(128)(4,1)}), s8[4194304]{0:T(1024)(128)(4,1)S(1)}, s32[]{:S(2)}) async-start(s8[16777216]{0:T(1024)(128)(4,1)} %bitcast.53), calls=%async_computation.5 | async-start | bytes 8388608
  793.3 20.0 %slice-start.3 = ((s8[16777216]{0:T(1024)(128)(4,1)}), s8[4194304]{0:T(1024)(128)(4,1)S(1)}, s32[]{:S(2)}) async-start(s8[16777216]{0:T(1024)(128)(4,1)} %bitcast.53), calls=%async_computation.6 | async-start | bytes 8388608
Sparse Core Ops, SparseCore 0:
  63.8 288.2 all-gather.4
  353.9 325.4 all-gather.2
where the time goes:
time: 918 us; the launch traced here: 913 us
  waiting for transfers between devices  633 us (69%)
  matrix products  156 us (17%)
  other arithmetic  55.5 us (6%)
  local copies, waits for them, and re-layouts  45.9 us (5%)
  between operations  13.7 us (1%)
    all_to_all x1, waiting for transfers between devices, relay_columns(): lax.all_to_all(gathered, 'col', split_axis=1, concat_axis=1, tiled=True)  302 us
    all_gather x1, waiting for transfers between devices, relay_columns(): gathered = lax.all_gather(paired, 'row', axis=1, tiled=True)  285 us
    dot_general x3, matrix products, contribute(): jnp.einsum('kro,co->krc', row_slices[left_index][:perturbations], column_...  97.3 us
    dot_general x3, matrix products, contribute(): jnp.einsum('ro,kco->krc', row_slices[right_index][perturbations], column_...  59 us
    ppermute x1, waiting for transfers between devices, partner(): return lax.ppermute(value, axis, pairs)  45.9 us
    convert_element_type x2, other arithmetic, split_slices(): trailing = lax.optimization_barrier(remainder.astype(jnp.bfloat16))  25.8 us
    all_gather x1, local copies, waits for them, and re-layouts, relay_columns(): gathered = lax.all_gather(paired, 'row', axis=1, tiled=True)  21.6 us
  transfers between devices with their start and end apart: 4, of which 3 were waited for; matrix products, arithmetic and copies ran while one was open for 6% of the time, Pallas kernels for 0%

commit v1 on v0

--- a/solution.py
+++ b/solution.py
@@ -4,6 +4,16 @@
 from jax.sharding import PartitionSpec as P
 
 SLICE_PAIRS = ((0, 0), (0, 1), (1, 0))
+
+
+def gather_by_hops(shard, axis, along):
+    peers = lax.axis_size(axis)
+    moving, pieces = (shard, [shard])
+    for _ in range(peers - 1):
+        moving = lax.ppermute(moving, axis, [(i, (i + 1) % peers) for i in range(peers)])
+        pieces.insert(0, moving)
+    line = jnp.concatenate(pieces, axis=along)
+    return jnp.roll(line, (lax.axis_index(axis) + 1) * shard.shape[along], axis=along)
 
 
 def partner(value, axis, stride):
@@ -54,7 +64,7 @@
     leading = jnp.where(even_first, own_first, partner_second)
     trailing = jnp.where(even_first, partner_second, own_first)
     paired = jnp.concatenate([leading, trailing], axis=1)
-    gathered = lax.all_gather(paired, "row", axis=1, tiled=True)
+    gathered = gather_by_hops(paired, "row", 1)
     regrouped = lax.all_to_all(gathered, "col", split_axis=1, concat_axis=1, tiled=True)
     shaped = regrouped.reshape(perturbations + 1, 2, rows_total, half_rows, orbitals)
     flipped = shaped[:, ::-1]

time: 918 us -> 861 us (0.938)
  waiting for transfers between devices: 633 us -> 534 us
  local copies, waits for them, and re-layouts: 45.9 us -> 91.7 us
    all_gather x1 -> x0, waiting for transfers between devices: 285 us -> none  [relay_columns(): gathered = lax.all_gather(paired, 'row', axis=1, tiled=True)]
    ppermute x0 -> x3, waiting for transfers between devices: none -> 270 us  [gather_by_hops(): lax.ppermute(moving, axis, [(i, (i + 1) % peers) for i in range(peers)])]
    all_to_all x1, waiting for transfers between devices: 302 us -> 184 us  [relay_columns(): lax.all_to_all(gathered, 'col', split_axis=1, concat_axis=1, tiled=True)]
    unnamed x14 -> x29, local copies, waits for them, and re-layouts: 9.03 us -> 46.7 us
    ppermute x1, waiting for transfers between devices: 45.9 us -> 80.3 us  [partner(): return lax.ppermute(value, axis, pairs)]
    dynamic_slice x0 -> x2, local copies, waits for them, and re-layouts: none -> 28.4 us  [gather_by_hops(): jnp.roll(line, (lax.axis_index(axis) + 1) * shard.shape[along], axis=along)]
    all_gather x1 -> x0, local copies, waits for them, and re-layouts: 21.6 us -> none  [relay_columns(): gathered = lax.all_gather(paired, 'row', axis=1, tiled=True)]
  transfers between devices with their start and end apart: 4 -> 6, of which waited for: 3 -> 5; matrix products, arithmetic and copies ran while one was open for 6% -> 11% of each run, Pallas kernels for 0% -> 0%
where the time goes in v1:
time: 861 us; the launch traced here: 855 us
  waiting for transfers between devices  534 us (62%)
  matrix products  153 us (18%)
  local copies, waits for them, and re-layouts  91.7 us (11%)
  other arithmetic  51.4 us (6%)
  between operations  13.8 us (2%)
  starting transfers between devices  10.8 us (1%)
    ppermute x3, waiting for transfers between devices, gather_by_hops(): lax.ppermute(moving, axis, [(i, (i + 1) % peers) for i in range(peers)])  270 us
    all_to_all x1, waiting for transfers between devices, relay_columns(): lax.all_to_all(gathered, 'col', split_axis=1, concat_axis=1, tiled=True)  184 us
    dot_general x3, matrix products, contribute(): jnp.einsum('kro,co->krc', row_slices[left_index][:perturbations], column_...  96.5 us
    ppermute x1, waiting for transfers between devices, partner(): return lax.ppermute(value, axis, pairs)  80.3 us
    dot_general x3, matrix products, contribute(): jnp.einsum('ro,kco->krc', row_slices[right_index][perturbations], column_...  56.5 us
    unnamed x29, local copies, waits for them, and re-layouts  46.7 us
    dynamic_slice x2, local copies, waits for them, and re-layouts, gather_by_hops(): jnp.roll(line, (lax.axis_index(axis) + 1) * shard.shape[along], axis=along)  28.4 us
    convert_element_type x2, other arithmetic, split_slices(): trailing = lax.optimization_barrier(remainder.astype(jnp.bfloat16))  23.2 us
  transfers between devices with their start and end apart: 6, of which 5 were waited for; matrix products, arithmetic and copies ran while one was open for 11% of the time, Pallas kernels for 0%

profile of v1, /device:TPU:0, one launch (start us, length us, event | category | flops | bytes accessed | tf_op | source)
XLA Modules:
  0.0 854.9 jit_solution(3209215302972781116)
XLA Ops:
  6.5 0.0 all-gather.2.cloned.1.call-start
  6.5 4.9 pad_maximum_fusion
  11.4 0.0 all-gather.2.cloned.1.call-update
  11.4 1.7 fusion.7
  13.1 3.1 collective-permute-start
  16.2 80.3 %collective-permute-done = f32[4,128,1024]{2,1,0:T(8,128)} collective-permute-done((f32[4,128,1024]{2,1,0:T(8,128)S(1)}, f32[4,128,1024]{2,1,0:T(8,128)}, u32[]{:S(2)}, u32[]{:S(2)}) %collective-permute-start) | collective-permute-done | bytes 2097184 | tf_op jit(solution)/shard_map/ppermute | solution.py:22
  96.4 0.0 copy-done.7
  96.5 3.1 broadcast_select_fusion.1
  99.6 1.4 copy-done.3
  101.0 0.6 pad_maximum_fusion.1
  101.6 1.6 collective-permute-start.1
  103.1 89.7 %collective-permute-done.1 = f32[4,256,1024]{2,1,0:T(8,128)S(1)} collective-permute-done((f32[4,256,1024]{2,1,0:T(8,128)S(1)}, f32[4,256,1024]{2,1,0:T(8,128)S(1)}, u32[]{:S(2)}, u32[]{:S(2)}) %collective-permute-start.1) | collective-permute-done | bytes 4194336 | tf_op jit(solution)/shard_map/ppermute | solution.py:13
  192.8 2.0 copy-done.5
  194.8 0.0 collective-permute-start.2
  194.8 90.5 %collective-permute-done.2 = f32[4,256,1024]{2,1,0:T(8,128)} collective-permute-done((f32[4,256,1024]{2,1,0:T(8,128)S(1)}, f32[4,256,1024]{2,1,0:T(8,128)}, u32[]{:S(2)}, u32[]{:S(2)}) %collective-permute-start.2) | collective-permute-done | bytes 4194336 | tf_op jit(solution)/shard_map/ppermute | solution.py:13
  285.3 0.0 collective-permute-start.3
  285.3 89.8 %collective-permute-done.3 = f32[4,256,1024]{2,1,0:T(8,128)} collective-permute-done((f32[4,256,1024]{2,1,0:T(8,128)}, f32[4,256,1024]{2,1,0:T(8,128)}, u32[]{:S(2)}, u32[]{:S(2)}) %collective-permute-start.3) | collective-permute-done | bytes 4194336 | tf_op jit(solution)/shard_map/ppermute | solution.py:13
  375.1 4.8 constant_dynamic-update-slice_fusion.9
  379.9 4.9 constant_dynamic-update-slice_fusion.8
  384.7 2.3 constant_dynamic-update-slice_fusion.7
  387.0 0.0 copy-done.4
  387.0 1.6 constant_dynamic-update-slice_fusion.6
  388.6 1.5 constant_dynamic-update-slice_fusion.5
  390.0 4.8 constant_dynamic-update-slice_fusion.4
  394.8 4.8 constant_dynamic-update-slice_fusion.3
  399.6 2.3 constant_dynamic-update-slice_fusion.2
  402.0 1.5 constant_dynamic-update-slice_fusion.1
  403.5 1.5 constant_dynamic-update-slice_fusion
  405.0 6.6 constant_dynamic-slice_fusion
  411.5 21.9 %copy.8 = f32[4,1024,1024]{2,0,1:T(4,128)} copy(f32[4,1024,1024]{2,1,0:T(8,128)S(1)} %constant_dynamic-slice_fusion) | data formatting | bytes 33554432 | tf_op jit(solution)/shard_map/jit(_roll_dynamic)/dynamic_slice | solution.py:16
  433.4 6.2 all-to-all-start
  439.6 183.9 %all-to-all-done = f32[4,1024,1024]{2,0,1:T(4,128)} async-done(((f32[4,1024,1024]{2,0,1:T(4,128)}), f32[4,1024,1024]{2,0,1:T(4,128)}, u32[]{:S(2)}, u32[]{:S(2)}) %all-to-all-start) | async-done | bytes 16777248 | tf_op jit(solution)/shard_map/all_to_all | solution.py:68
  623.5 15.2 %copy.10 = f32[4,2,4,128,1024]{4,3,1,2,0:T(8,128)S(1)} copy(f32[4,2,4,128,1024]{4,0,3,2,1:T(4,128)} %bitcast.1) | data formatting | bytes 33554432 | tf_op jit(solution)/shard_map/reshape | solution.py:69
  638.7 3.4 reverse_select_fusion
  642.1 2.4 bitcast_convert_fusion
  644.6 3.2 copy-done.2
  647.8 6.3 fusion.2
  654.1 12.1 %convert_element_type.18 = bf16[4,2048,1024]{2,1,0:T(8,128)(2,1)S(1)} convert(f32[4,2048,1024]{2,1,0:T(8,128)} %all-gather.2.cloned.1.call-done) | non-fusion elementwise | flops 8388608 | bytes 50331648 | tf_op jit(solution)/shard_map/convert_element_type | solution.py:26
  666.2 5.8 copy-done
  672.0 19.1 %fusion.4 = f32[3,1024,2048]{1,2,0:T(8,128)} fusion(bf16[4,1024,1024]{2,1,0:T(8,128)(2,1)} %fusion.2, bf16[4,2048,1024]{2,1,0:T(8,128)(2,1)S(1)} %convert_element_type.18), kind=kOutput, calls=%fused_computation.19 | convolution fusion | flops 12884901888 | bytes 37748736 | tf_op jit(solution)/shard_map/ro,kco->krc/dot_general | solution.py:43
  691.2 21.8 %fusion.8 = f32[3,2048,1024]{2,1,0:T(8,128)} fusion(bf16[4,2048,1024]{2,1,0:T(8,128)(2,1)} %copy-done, bf16[4,1024,1024]{2,1,0:T(8,128)(2,1)} %fusion.2), kind=kOutput, calls=%fused_computation.24 | convolution fusion | flops 12884901888 | bytes 44040192 | tf_op jit(solution)/shard_map/kro,co->krc/dot_general | solution.py:37
  713.0 0.0 slice-done.1
  713.0 18.6 %fusion.5 = f32[3,1024,2048]{1,2,0:T(8,128)} fusion(bf16[4,1024,1024]{2,1,0:T(8,128)(2,1)S(1)} %bitcast.54, bf16[4,2048,1024]{2,1,0:T(8,128)(2,1)} %copy-done), kind=kOutput, calls=%fused_computation.20 | convolution fusion | flops 12884901888 | bytes 37748736 | tf_op jit(solution)/shard_map/ro,kco->krc/dot_general | solution.py:43
  731.5 21.2 %fusion.9 = f32[3,2048,1024]{2,1,0:T(8,128)} fusion(bf16[4,2048,1024]{2,1,0:T(8,128)(2,1)} %copy-done, bf16[4,1024,1024]{2,1,0:T(8,128)(2,1)S(1)} %bitcast.54), kind=kOutput, calls=%fused_computation.26 | convolution fusion | flops 12884901888 | bytes 44040192 | tf_op jit(solution)/shard_map/kro,co->krc/dot_general | solution.py:37
  752.7 16.9 %subtract_convert_fusion = bf16[4,2048,1024]{2,1,0:T(8,128)(2,1)S(1)} fusion(f32[4,2048,1024]{2,1,0:T(8,128)} %all-gather.2.cloned.1.call-done, bf16[4,2048,1024]{2,1,0:T(8,128)(2,1)} %copy-done), kind=kLoop, calls=%fused_computation | loop fusion | flops 25165824 | bytes 67108864 | tf_op jit(solution)/shard_map/convert_element_type | solution.py:28
  769.6 5.8 copy-done.1
  775.5 18.8 %fusion.3 = f32[3,1024,2048]{1,2,0:T(8,128)} fusion(bf16[4,1024,1024]{2,1,0:T(8,128)(2,1)} %copy-done.2, bf16[4,2048,1024]{2,1,0:T(8,128)(2,1)S(1)} %subtract_convert_fusion), kind=kOutput, calls=%fused_computation.16 | convolution fusion | flops 12884901888 | bytes 37748736 | tf_op jit(solution)/shard_map/ro,kco->krc/dot_general | solution.py:43
  794.3 53.5 %bitcast_add_fusion = f32[3,2048,1024]{2,1,0:T(8,128)} fusion(f32[3,1024,2048]{1,2,0:T(8,128)} %fusion.4, f32[3,1024,2048]{1,2,0:T(8,128)} %fusion.3, f32[3,2048,1024]{2,1,0:T(8,128)} %fusion.8, f32[3,2048,1024]{2,1,0:T(8,128)} %fusion.9, f32[3,1024,2048]{1,2,0:T(8,128)} %fusion.5, bf16[4,2048,1024]{2,1,0:T(8,128)(2,1)} %copy-done.1, ...), kind=kOutput, calls=%fused_computation.1 | convolution fusion | flops 12916359168 | bytes 169869312 | tf_op jit(solution)/shard_map/kro,co->krc/dot_general | solution.py:37
  (14 shorter events, 0.0 us)
Async XLA Ops:
  6.5 89.9 %copy-start.7 = (f32[256,1024]{1,0:T(8,128)S(1)}, f32[256,1024]{1,0:T(8,128)}, u32[]{:S(2)}) copy-start(f32[256,1024]{1,0:T(8,128)} %param.3) | copy-start | bytes 3145732
  6.5 647.5 %all-gather.2.cloned.1.call-start = ((), (), s32[]{:S(2)}) async-start(), calls=%async_computation.1 | async-start | bytes 37748736 | tf_op jit(solution)/shard_map/all_gather | solution.py:83
  13.1 83.4 %collective-permute-start = (f32[4,128,1024]{2,1,0:T(8,128)S(1)}, f32[4,128,1024]{2,1,0:T(8,128)}, u32[]{:S(2)}, u32[]{:S(2)}) collective-permute-start(f32[4,128,1024]{2,1,0:T(8,128)S(1)} %fusion.7), channel_id=1, source_target_pairs={{0,4},{1,5},{2,6},{3,7},{4,0},{5,1},{6,2},{7,3},{8,12},{9,13},{10,... | collective-permute-start | bytes 6291464 | tf_op jit(solution)/shard_map/ppermute | solution.py:22
  99.6 1.4 copy-start.3
  101.6 91.2 %collective-permute-start.1 = (f32[4,256,1024]{2,1,0:T(8,128)S(1)}, f32[4,256,1024]{2,1,0:T(8,128)S(1)}, u32[]{:S(2)}, u32[]{:S(2)}) collective-permute-start(f32[4,256,1024]{2,1,0:T(8,128)S(1)} %pad_maximum_fusion.1), channel_id=1, source_target_pairs={{0,8},{8,16},{16,24},{24,0},{1,9},{9,17},{17,25},{25,1},{2,10},{10... | collective-permute-start | bytes 12582920 | tf_op jit(solution)/shard_map/ppermute | solution.py:13
  192.8 2.0 copy-start.5
  194.8 90.5 %collective-permute-start.2 = (f32[4,256,1024]{2,1,0:T(8,128)S(1)}, f32[4,256,1024]{2,1,0:T(8,128)}, u32[]{:S(2)}, u32[]{:S(2)}) collective-permute-start(f32[4,256,1024]{2,1,0:T(8,128)S(1)} %collective-permute-done.1), channel_id=1, source_target_pairs={{0,8},{8,16},{16,24},{24,0},{1,9},{9,17},{17,25},{25,1},{2,10},{10... | collective-permute-start | bytes 12582920 | tf_op jit(solution)/shard_map/ppermute | solution.py:13
  285.3 89.8 %collective-permute-start.3 = (f32[4,256,1024]{2,1,0:T(8,128)}, f32[4,256,1024]{2,1,0:T(8,128)}, u32[]{:S(2)}, u32[]{:S(2)}) collective-permute-start(f32[4,256,1024]{2,1,0:T(8,128)} %collective-permute-done.2), channel_id=1, source_target_pairs={{0,8},{8,16},{16,24},{24,0},{1,9},{9,17},{17,25},{25,1},{2,10},{10... | collective-permute-start | bytes 12582920 | tf_op jit(solution)/shard_map/ppermute | solution.py:13
  285.3 99.4 %copy-start.6 = (f32[4,256,1024]{2,1,0:T(8,128)S(1)}, f32[4,256,1024]{2,1,0:T(8,128)}, u32[]{:S(2)}) copy-start(f32[4,256,1024]{2,1,0:T(8,128)} %copy-done.5) | copy-start | bytes 12582916
  285.3 101.7 %copy-start.4 = (f32[4,128,1024]{2,1,0:T(8,128)S(1)}, f32[4,128,1024]{2,1,0:T(8,128)}, u32[]{:S(2)}) copy-start(f32[4,128,1024]{2,1,0:T(8,128)} %copy-done.3) | copy-start | bytes 6291460
  433.4 190.1 %all-to-all-start = ((f32[4,1024,1024]{2,0,1:T(4,128)}), f32[4,1024,1024]{2,0,1:T(4,128)}, u32[]{:S(2)}, u32[]{:S(2)}) async-start(f32[4,1024,1024]{2,0,1:T(4,128)} %copy.8), calls=%async_computation | async-start | bytes 33554432 | tf_op jit(solution)/shard_map/all_to_all | solution.py:68
  644.6 3.2 copy-start.2
  666.2 5.8 copy-start
  672.0 40.9 %slice-start = ((s8[8388608]{0:T(1024)(128)(4,1)}), s8[4194304]{0:T(1024)(128)(4,1)S(1)}, s32[]{:S(2)}) async-start(s8[8388608]{0:T(1024)(128)(4,1)} %bitcast.53), calls=%async_computation.2 | async-start | bytes 8388608
  691.1 21.8 %slice-start.1 = ((s8[8388608]{0:T(1024)(128)(4,1)}), s8[4194304]{0:T(1024)(128)(4,1)S(1)}, s32[]{:S(2)}) async-start(s8[8388608]{0:T(1024)(128)(4,1)} %bitcast.53), calls=%async_computation.3 | async-start | bytes 8388608
  769.6 5.8 copy-start.1
Sparse Core Ops, SparseCore 0:
  11.6 197.7 all-gather.1
